TPU v7x, 8 devices: a whole 2x2x1 slice. The times are simulated.
8 devices in a mesh: dp: 2 (over z, y), sp: 4 (over x, core).
Axes of the slice: x: 2, y: 2, z: 1, core: 2. Of those that a mesh axis runs over, the one named last changes fastest.
Arguments:
- hidden: bfloat16 [24576, 896], P(('dp', 'sp')), parts along dimension 0
- tok_perm: int32 [24576], P(('dp', 'sp')), parts along dimension 0
- send_off: int32 [32], P(('dp', 'sp')), parts along dimension 0
- send_len: int32 [32], P(('dp', 'sp')), parts along dimension 0
- recv_off: int32 [32], P(('dp', 'sp')), parts along dimension 0
- recv_len: int32 [32], P(('dp', 'sp')), parts along dimension 0
- recv_doc: int32 [12288], P(('dp', 'sp')), parts along dimension 0
- recv_pos: int32 [12288], P(('dp', 'sp')), parts along dimension 0
- g_attn: bfloat16 [896], replicated
- w_q: bfloat16 [896, 14, 64], replicated
- w_k: bfloat16 [896, 2, 64], replicated
- w_v: bfloat16 [896, 2, 64], replicated
- w_o: bfloat16 [14, 64, 896], replicated
- g_mlp: bfloat16 [896], replicated
- w_gate: bfloat16 [896, 4864], replicated
- w_up: bfloat16 [896, 4864], replicated
- w_down: bfloat16 [4864, 896], replicated
Outputs:
- output: bfloat16 [24576, 896], P(('dp', 'sp')), parts along dimension 0
There are 2 independent parts. A program takes and returns all parts, laid end to end along the dimension named above; an argument that names none is the same for every part.
All inputs are finite; a program needn't handle non-finite values.
Results may differ from a plain program's by a relative error of at most 0.0108911.
Values are sent between devices in bfloat16 or wider.
A program may use at most 1 GiB of HBM per device.

v0:
```python
import jax
import jax.numpy as jnp
from jax import lax
from jax.sharding import PartitionSpec as P

Q_BLOCK = 128
ROPE_BASE = 500000.0
NORM_EPS = 1e-5


def rms_norm(rows_in, gain_vec):
    rows_f = rows_in.astype(jnp.float32)
    inv_rms = lax.rsqrt(jnp.mean(rows_f * rows_f, axis=-1, keepdims=True) + NORM_EPS)
    return (rows_f * inv_rms * gain_vec.astype(jnp.float32)).astype(jnp.bfloat16)


def rope(proj, positions):
    head_dim = proj.shape[-1]
    half_dim = head_dim // 2
    inv_freq = jnp.power(jnp.float32(ROPE_BASE), -2.0 * jnp.arange(half_dim, dtype=jnp.float32) / head_dim)
    angles = positions.astype(jnp.float32)[:, None, None] * inv_freq[None, None, :]
    cos_t = jnp.cos(angles)
    sin_t = jnp.sin(angles)
    lo_half = proj[..., :half_dim]
    hi_half = proj[..., half_dim:]
    return jnp.concatenate([lo_half * cos_t - hi_half * sin_t, hi_half * cos_t + lo_half * sin_t], axis=-1)


def attend(q_rot, k_rot, v_proj, doc_ids, positions):
    n_rows, n_kv, q_per_kv, head_dim = q_rot.shape
    n_blocks = n_rows // Q_BLOCK
    qk_scale = head_dim ** -0.5

    def one_block(blk_args):
        q_blk, doc_q, pos_q = blk_args
        scores = jnp.einsum('qkgd,skd->kgqs', q_blk, k_rot, preferred_element_type=jnp.float32) * qk_scale
        allowed = (doc_q[:, None] == doc_ids[None, :]) & (positions[None, :] <= pos_q[:, None])
        probs_bf = jax.nn.softmax(jnp.where(allowed, scores, -1e30), axis=-1).astype(jnp.bfloat16)
        return jnp.einsum('kgqs,skd->qkgd', probs_bf, v_proj, preferred_element_type=jnp.float32).astype(jnp.bfloat16)

    blocks_out = lax.map(one_block, (q_rot.reshape(n_blocks, Q_BLOCK, n_kv, q_per_kv, head_dim), doc_ids.reshape(n_blocks, Q_BLOCK), positions.reshape(n_blocks, Q_BLOCK)))
    return blocks_out.reshape(n_rows, n_kv, q_per_kv, head_dim)


def layer(dest_rows, doc_ids, positions, g_attn, w_q, w_k, w_v, w_o, g_mlp, w_gate, w_up, w_down):
    n_rows, model_dim = dest_rows.shape
    n_heads = w_q.shape[1]
    head_dim = w_q.shape[2]
    n_kv = w_k.shape[1]
    normed = rms_norm(dest_rows, g_attn)
    q_proj = jnp.einsum('td,dhe->the', normed, w_q, preferred_element_type=jnp.float32)
    k_proj = jnp.einsum('td,dhe->the', normed, w_k, preferred_element_type=jnp.float32)
    v_proj = jnp.einsum('td,dhe->the', normed, w_v, preferred_element_type=jnp.float32).astype(jnp.bfloat16)
    q_rot = rope(q_proj, positions).astype(jnp.bfloat16).reshape(n_rows, n_kv, n_heads // n_kv, head_dim)
    k_rot = rope(k_proj, positions).astype(jnp.bfloat16)
    attn_heads = attend(q_rot, k_rot, v_proj, doc_ids, positions)
    attn_out = jnp.einsum('qkgd,kgde->qe', attn_heads, w_o.reshape(n_kv, n_heads // n_kv, head_dim, model_dim), preferred_element_type=jnp.float32).astype(jnp.bfloat16)
    resid_mid = (dest_rows.astype(jnp.float32) + attn_out.astype(jnp.float32)).astype(jnp.bfloat16)
    normed_mlp = rms_norm(resid_mid, g_mlp)
    gate_proj = jnp.dot(normed_mlp, w_gate, preferred_element_type=jnp.float32)
    up_proj = jnp.dot(normed_mlp, w_up, preferred_element_type=jnp.float32)
    hidden_act = (jax.nn.silu(gate_proj) * up_proj).astype(jnp.bfloat16)
    down_proj = jnp.dot(hidden_act, w_down, preferred_element_type=jnp.float32).astype(jnp.bfloat16)
    return (resid_mid.astype(jnp.float32) + down_proj.astype(jnp.float32)).astype(jnp.bfloat16)


def solution(mesh):
    row_spec = P(('dp', 'sp'), None)
    vec_spec = P(('dp', 'sp'))
    rep_spec = P()

    def per_device(hidden, tok_perm, send_off, send_len, recv_off, recv_len, recv_doc, recv_pos, g_attn, w_q, w_k, w_v, w_o, g_mlp, w_gate, w_up, w_down):
        n_tok, model_dim = hidden.shape
        n_cap = recv_doc.shape[0]
        group_devs = send_off.shape[0]
        zero_val = jnp.zeros((), hidden.dtype)
        pair_row = jnp.arange(n_cap)[None, :]
        dev_base = jnp.arange(group_devs)[None, :] * n_cap
        send_idx = jnp.minimum(send_off[:, None] + pair_row, n_tok - 1).reshape(-1)
        send_buf = jnp.take(hidden, jnp.take(tok_perm, send_idx), axis=0).reshape(group_devs, n_cap, model_dim)
        recv_buf = lax.all_to_all(send_buf, 'sp', 0, 0, tiled=True).reshape(group_devs * n_cap, model_dim)
        slot_idx = jnp.arange(n_cap)[:, None]
        in_run = (slot_idx >= recv_off[None, :]) & (slot_idx < (recv_off + recv_len)[None, :])
        flat_pos = jnp.sum(jnp.where(in_run, dev_base + slot_idx - recv_off[None, :], 0), axis=1)
        dest_rows = jnp.take(recv_buf, flat_pos, axis=0)
        layer_rows = layer(dest_rows, recv_doc, recv_pos, g_attn, w_q, w_k, w_v, w_o, g_mlp, w_gate, w_up, w_down)
        back_idx = jnp.minimum(recv_off[:, None] + pair_row, n_cap - 1).reshape(-1)
        back_buf = jnp.take(layer_rows, back_idx, axis=0).reshape(group_devs, n_cap, model_dim)
        back_recv = lax.all_to_all(back_buf, 'sp', 0, 0, tiled=True).reshape(group_devs * n_cap, model_dim)
        inv_perm = jnp.argsort(tok_perm)[:, None]
        in_back = (inv_perm >= send_off[None, :]) & (inv_perm < (send_off + send_len)[None, :])
        back_pos = jnp.sum(jnp.where(in_back, dev_base + inv_perm - send_off[None, :], 0), axis=1)
        was_sent = jnp.any(in_back, axis=1)
        return jnp.where(was_sent[:, None], jnp.take(back_recv, back_pos, axis=0), zero_val)

    return jax.shard_map(per_device, mesh=mesh, in_specs=(row_spec,) + (vec_spec,) * 7 + (rep_spec,) * 9, out_specs=row_spec, check_vma=False)
```

profile of v0, /device:TPU:0, one launch (start us, length us, event | category | flops | bytes accessed | tf_op | source)
XLA Modules:
  0.0 717.9 jit_solution(15730631778921620042)
XLA Ops:
  1.0 34.3 %gather_fusion = s32[6144]{0:T(1024)S(1)} fusion(s32[3072]{0:T(1024)S(1)} %copy-done.2, s32[6144]{0:T(1024)S(1)} %broadcast_clamp_fusion.2), kind=kCustom, calls=%fused_computation | custom fusion | bytes 73728 | tf_op jit(solution)/shard_map/jit(_take)/gather | solution.py:80
  35.5 32.5 %gather_fusion.1 = bf16[6144,896]{1,0:T(8,128)(2,1)} fusion(bf16[3072,896]{1,0:T(8,128)(2,1)} %param.19, s32[6144]{0:T(1024)S(1)} %broadcast_clamp_fusion.1), kind=kCustom, calls=%fused_computation.1 | custom fusion | bytes 22044672 | tf_op jit(solution)/shard_map/jit(_take)/gather | solution.py:80
  68.0 10.0 %broadcast_select_fusion = bf16[4,1536,896]{2,1,0:T(8,128)(2,1)} fusion(bf16[4,1536,896]{2,1,0:T(8,128)(2,1)} %bitcast.114, pred[4,1536]{1,0:T(4,128)(4,1)S(1)} %compare_and_fusion.2), kind=kLoop, calls=%fused_computation.40 | loop fusion | flops 5505024 | bytes 22026240 | tf_op jit(solution)/shard_map/jit(_take)/select_n | solution.py:80
  78.1 6.9 all-to-all-start
  87.8 119.0 %all-to-all-done = bf16[4,1536,896]{2,1,0:T(8,128)(2,1)} async-done(((bf16[4,1536,896]{2,1,0:T(8,128)(2,1)}), bf16[4,1536,896]{2,1,0:T(8,128)(2,1)}, u32[]{:S(2)}, u32[]{:S(2)}) %all-to-all-start) | async-done | bytes 11010080 | tf_op jit(solution)/shard_map/all_to_all | solution.py:81
  206.8 12.6 %gather_fusion.2 = bf16[1536,896]{1,0:T(8,128)(2,1)} fusion(bf16[6144,896]{1,0:T(8,128)(2,1)} %bitcast.14, s32[2048]{0:T(1024)S(1)} %pad_clamp_fusion), kind=kCustom, calls=%fused_computation.2 | custom fusion | bytes 5511168 | tf_op jit(solution)/shard_map/jit(_take)/gather | solution.py:85
  248.7 187.7 %while.10 = (s32[]{:T(128)}, bf16[12,128,2,7,64]{1,4,3,2,0:T(8,128)(2,1)}, s32[12,128]{1,0:T(8,128)S(1)}, s32[1536]{0:T(1024)S(1)}, s32[1536]{0:T(1024)S(1)}, /*...) while((s32[]{:T(128)}, ...), condition=%wide.region_8.9_spmd, body=%wide.region_5.8_spmd.sunk | while | flops 721864192 | bytes 23689320 | solution.py:41
  249.0 8.7 %fusion.92 = (f32[2,7,128]{2,1,0:T(8,128)S(1)}, f32[2,7,128,1536]{3,2,1,0:T(8,128)}) fusion(pred[128,1536]{1,0:T(8,128)(4,1)S(1)} %compare_and_fusion.7, bf16[1536,2,64]{0,2,1:T(8,128)(2,1)S(1)} %get-tuple-element.193, bf16[12,128,2,7,64]{1,4,3,2,0:T(8,128)(2,1)} %get-tuple-element.192, s32[]{:T(128)} %get-tuple-element.176), kind=kOutput, calls=%fused_computation.110.clone.1 | convolution fusion | flops 363333120 | bytes 11836928 | tf_op jit(solution)/shard_map/while/body/eval_jaxpr/sub | solution.py:38
  264.6 8.7 %fusion.92 = (f32[2,7,128]{2,1,0:T(8,128)S(1)}, f32[2,7,128,1536]{3,2,1,0:T(8,128)}) fusion(pred[128,1536]{1,0:T(8,128)(4,1)S(1)} %compare_and_fusion.7, bf16[1536,2,64]{0,2,1:T(8,128)(2,1)S(1)} %get-tuple-element.193, bf16[12,128,2,7,64]{1,4,3,2,0:T(8,128)(2,1)} %get-tuple-element.192, s32[]{:T(128)} %get-tuple-element.176), kind=kOutput, calls=%fused_computation.110.clone.1 | convolution fusion | flops 363333120 | bytes 11836928 | tf_op jit(solution)/shard_map/while/body/eval_jaxpr/sub | solution.py:38
  273.3 6.7 fusion.93
  280.3 8.7 %fusion.92 = (f32[2,7,128]{2,1,0:T(8,128)S(1)}, f32[2,7,128,1536]{3,2,1,0:T(8,128)}) fusion(pred[128,1536]{1,0:T(8,128)(4,1)S(1)} %compare_and_fusion.7, bf16[1536,2,64]{0,2,1:T(8,128)(2,1)S(1)} %get-tuple-element.193, bf16[12,128,2,7,64]{1,4,3,2,0:T(8,128)(2,1)} %get-tuple-element.192, s32[]{:T(128)} %get-tuple-element.176), kind=kOutput, calls=%fused_computation.110.clone.1 | convolution fusion | flops 363333120 | bytes 11836928 | tf_op jit(solution)/shard_map/while/body/eval_jaxpr/sub | solution.py:38
  289.0 6.7 fusion.93
  295.9 8.7 %fusion.92 = (f32[2,7,128]{2,1,0:T(8,128)S(1)}, f32[2,7,128,1536]{3,2,1,0:T(8,128)}) fusion(pred[128,1536]{1,0:T(8,128)(4,1)S(1)} %compare_and_fusion.7, bf16[1536,2,64]{0,2,1:T(8,128)(2,1)S(1)} %get-tuple-element.193, bf16[12,128,2,7,64]{1,4,3,2,0:T(8,128)(2,1)} %get-tuple-element.192, s32[]{:T(128)} %get-tuple-element.176), kind=kOutput, calls=%fused_computation.110.clone.1 | convolution fusion | flops 363333120 | bytes 11836928 | tf_op jit(solution)/shard_map/while/body/eval_jaxpr/sub | solution.py:38
  304.6 6.7 fusion.93
  311.6 8.7 %fusion.92 = (f32[2,7,128]{2,1,0:T(8,128)S(1)}, f32[2,7,128,1536]{3,2,1,0:T(8,128)}) fusion(pred[128,1536]{1,0:T(8,128)(4,1)S(1)} %compare_and_fusion.7, bf16[1536,2,64]{0,2,1:T(8,128)(2,1)S(1)} %get-tuple-element.193, bf16[12,128,2,7,64]{1,4,3,2,0:T(8,128)(2,1)} %get-tuple-element.192, s32[]{:T(128)} %get-tuple-element.176), kind=kOutput, calls=%fused_computation.110.clone.1 | convolution fusion | flops 363333120 | bytes 11836928 | tf_op jit(solution)/shard_map/while/body/eval_jaxpr/sub | solution.py:38
  327.2 8.7 %fusion.92 = (f32[2,7,128]{2,1,0:T(8,128)S(1)}, f32[2,7,128,1536]{3,2,1,0:T(8,128)}) fusion(pred[128,1536]{1,0:T(8,128)(4,1)S(1)} %compare_and_fusion.7, bf16[1536,2,64]{0,2,1:T(8,128)(2,1)S(1)} %get-tuple-element.193, bf16[12,128,2,7,64]{1,4,3,2,0:T(8,128)(2,1)} %get-tuple-element.192, s32[]{:T(128)} %get-tuple-element.176), kind=kOutput, calls=%fused_computation.110.clone.1 | convolution fusion | flops 363333120 | bytes 11836928 | tf_op jit(solution)/shard_map/while/body/eval_jaxpr/sub | solution.py:38
  342.9 8.7 %fusion.92 = (f32[2,7,128]{2,1,0:T(8,128)S(1)}, f32[2,7,128,1536]{3,2,1,0:T(8,128)}) fusion(pred[128,1536]{1,0:T(8,128)(4,1)S(1)} %compare_and_fusion.7, bf16[1536,2,64]{0,2,1:T(8,128)(2,1)S(1)} %get-tuple-element.193, bf16[12,128,2,7,64]{1,4,3,2,0:T(8,128)(2,1)} %get-tuple-element.192, s32[]{:T(128)} %get-tuple-element.176), kind=kOutput, calls=%fused_computation.110.clone.1 | convolution fusion | flops 363333120 | bytes 11836928 | tf_op jit(solution)/shard_map/while/body/eval_jaxpr/sub | solution.py:38
  358.5 8.7 %fusion.92 = (f32[2,7,128]{2,1,0:T(8,128)S(1)}, f32[2,7,128,1536]{3,2,1,0:T(8,128)}) fusion(pred[128,1536]{1,0:T(8,128)(4,1)S(1)} %compare_and_fusion.7, bf16[1536,2,64]{0,2,1:T(8,128)(2,1)S(1)} %get-tuple-element.193, bf16[12,128,2,7,64]{1,4,3,2,0:T(8,128)(2,1)} %get-tuple-element.192, s32[]{:T(128)} %get-tuple-element.176), kind=kOutput, calls=%fused_computation.110.clone.1 | convolution fusion | flops 363333120 | bytes 11836928 | tf_op jit(solution)/shard_map/while/body/eval_jaxpr/sub | solution.py:38
  367.2 6.7 fusion.93
  374.1 8.7 %fusion.92 = (f32[2,7,128]{2,1,0:T(8,128)S(1)}, f32[2,7,128,1536]{3,2,1,0:T(8,128)}) fusion(pred[128,1536]{1,0:T(8,128)(4,1)S(1)} %compare_and_fusion.7, bf16[1536,2,64]{0,2,1:T(8,128)(2,1)S(1)} %get-tuple-element.193, bf16[12,128,2,7,64]{1,4,3,2,0:T(8,128)(2,1)} %get-tuple-element.192, s32[]{:T(128)} %get-tuple-element.176), kind=kOutput, calls=%fused_computation.110.clone.1 | convolution fusion | flops 363333120 | bytes 11836928 | tf_op jit(solution)/shard_map/while/body/eval_jaxpr/sub | solution.py:38
  382.8 6.7 fusion.93
  389.8 8.7 %fusion.92 = (f32[2,7,128]{2,1,0:T(8,128)S(1)}, f32[2,7,128,1536]{3,2,1,0:T(8,128)}) fusion(pred[128,1536]{1,0:T(8,128)(4,1)S(1)} %compare_and_fusion.7, bf16[1536,2,64]{0,2,1:T(8,128)(2,1)S(1)} %get-tuple-element.193, bf16[12,128,2,7,64]{1,4,3,2,0:T(8,128)(2,1)} %get-tuple-element.192, s32[]{:T(128)} %get-tuple-element.176), kind=kOutput, calls=%fused_computation.110.clone.1 | convolution fusion | flops 363333120 | bytes 11836928 | tf_op jit(solution)/shard_map/while/body/eval_jaxpr/sub | solution.py:38
  398.5 6.7 fusion.93
  405.4 8.7 %fusion.92 = (f32[2,7,128]{2,1,0:T(8,128)S(1)}, f32[2,7,128,1536]{3,2,1,0:T(8,128)}) fusion(pred[128,1536]{1,0:T(8,128)(4,1)S(1)} %compare_and_fusion.7, bf16[1536,2,64]{0,2,1:T(8,128)(2,1)S(1)} %get-tuple-element.193, bf16[12,128,2,7,64]{1,4,3,2,0:T(8,128)(2,1)} %get-tuple-element.192, s32[]{:T(128)} %get-tuple-element.176), kind=kOutput, calls=%fused_computation.110.clone.1 | convolution fusion | flops 363333120 | bytes 11836928 | tf_op jit(solution)/shard_map/while/body/eval_jaxpr/sub | solution.py:38
  421.0 8.7 %fusion.92 = (f32[2,7,128]{2,1,0:T(8,128)S(1)}, f32[2,7,128,1536]{3,2,1,0:T(8,128)}) fusion(pred[128,1536]{1,0:T(8,128)(4,1)S(1)} %compare_and_fusion.7, bf16[1536,2,64]{0,2,1:T(8,128)(2,1)S(1)} %get-tuple-element.193, bf16[12,128,2,7,64]{1,4,3,2,0:T(8,128)(2,1)} %get-tuple-element.192, s32[]{:T(128)} %get-tuple-element.176), kind=kOutput, calls=%fused_computation.110.clone.1 | convolution fusion | flops 363333120 | bytes 11836928 | tf_op jit(solution)/shard_map/while/body/eval_jaxpr/sub | solution.py:38
  429.7 6.7 fusion.93
  456.2 23.2 %fusion.51 = f32[1536,4864]{1,0:T(8,128)} fusion(bf16[896,4864]{1,0:T(8,128)(2,1)} %param.33, bf16[1536,896]{0,1:T(8,128)(2,1)S(1)} %get-tuple-element.102, f32[896]{0:T(1024)S(1)} %convert_element_type.69, f32[1536]{0:T(1024)S(1)} %add_rsqrt_fusion), kind=kOutput, calls=%fused_computation.63 | convolution fusion | flops 13393723392 | bytes 41362944 | tf_op jit(solution)/shard_map/dot_general | solution.py:60
  479.4 44.0 %fusion.47 = bf16[1536,896]{0,1:T(8,128)(2,1)} fusion(bf16[1536,896]{0,1:T(8,128)(2,1)} %copy-done.24, bf16[4864,896]{1,0:T(8,128)(2,1)} %param.35, f32[1536,4864]{1,0:T(8,128)} %fusion.51, bf16[896,4864]{1,0:T(8,128)(2,1)} %param.34, f32[896]{0:T(1024)S(1)} %convert_element_type.69, f32[1536]{0:T(1024)S(1)} %add_rsqrt_fusion), kind=kOutput, calls=%fused_computation.55 | convolution fusion | flops 26833649664 | bytes 52831744 | tf_op jit(solution)/shard_map/dot_general | solution.py:63
  526.7 26.5 %gather_fusion.3 = bf16[6144,896]{1,0:T(8,128)(2,1)} fusion(bf16[1536,896]{1,0:T(8,128)(2,1)S(1)} %copy.46, s32[6144]{0:T(1024)S(1)} %copy-done.10), kind=kCustom, calls=%fused_computation.3 | custom fusion | bytes 22044672 | tf_op jit(solution)/shard_map/jit(_take)/gather | solution.py:88
  553.2 10.0 %broadcast_select_fusion.1 = bf16[4,1536,896]{2,1,0:T(8,128)(2,1)} fusion(bf16[4,1536,896]{2,1,0:T(8,128)(2,1)} %bitcast.113, pred[4,1536]{1,0:T(4,128)(4,1)S(1)} %copy-done.11), kind=kLoop, calls=%fused_computation.41 | loop fusion | flops 5505024 | bytes 22026240 | tf_op jit(solution)/shard_map/jit(_take)/select_n | solution.py:88
  575.7 114.8 %all-to-all-done.1 = bf16[4,1536,896]{2,1,0:T(8,128)(2,1)} async-done(((bf16[4,1536,896]{2,1,0:T(8,128)(2,1)}), bf16[4,1536,896]{2,1,0:T(8,128)(2,1)}, u32[]{:S(2)}, u32[]{:S(2)}) %all-to-all-start.1) | async-done | bytes 11010080 | tf_op jit(solution)/shard_map/all_to_all | solution.py:89
  690.5 20.7 %gather_fusion.4 = bf16[3072,896]{1,0:T(8,128)(2,1)} fusion(bf16[6144,896]{1,0:T(8,128)(2,1)} %bitcast.28, s32[3072]{0:T(1024)S(1)} %broadcast_clamp_fusion.3), kind=kCustom, calls=%fused_computation.4 | custom fusion | bytes 11022336 | tf_op jit(solution)/shard_map/jit(_take)/gather | solution.py:94
  (133 shorter events, 111.2 us)
Async XLA Ops:
  0.0 448.4 %copy-start = (bf16[14,64,896]{2,1,0:T(8,128)(2,1)S(1)}, bf16[14,64,896]{2,1,0:T(8,128)(2,1)}, u32[]{:S(2)}) copy-start(bf16[14,64,896]{2,1,0:T(8,128)(2,1)} %param.31) | copy-start | bytes 4816900
  0.0 0.9 copy-start.2
  1.0 34.4 %copy-start.12 = (s32[4]{0:T(128)S(1)}, s32[4]{0:T(128)}, u32[]{:S(2)}) copy-start(s32[4]{0:T(128)} %param.21) | copy-start | bytes 52
  78.0 6.9 copy-start.15
  78.0 6.9 copy-start.8
  78.0 6.9 copy-start.16
  78.0 7.0 copy-start.14
  78.0 7.0 copy-start.22
  78.1 128.7 %all-to-all-start = ((bf16[4,1536,896]{2,1,0:T(8,128)(2,1)}), bf16[4,1536,896]{2,1,0:T(8,128)(2,1)}, u32[]{:S(2)}, u32[]{:S(2)}) async-start(bf16[4,1536,896]{2,1,0:T(8,128)(2,1)} %broadcast_select_fusion), calls=%async_computation | async-start | bytes 22020096 | tf_op jit(solution)/shard_map/all_to_all | solution.py:81
  85.1 0.5 copy-start.17
  219.4 7.5 %copy-start.20 = (bf16[896,2,64]{0,2,1:T(8,128)(2,1)S(1)}, bf16[896,2,64]{0,2,1:T(8,128)(2,1)}, u32[]{:S(2)}) copy-start(bf16[896,2,64]{0,2,1:T(8,128)(2,1)} %param.29) | copy-start | bytes 688132
  224.1 5.7 copy-start.4
  224.1 5.7 copy-start.19
  242.9 4.6 copy-start.5
  242.9 4.6 copy-start.21
  247.4 1.2 copy-start.6
  247.4 1.3 copy-start.7
  247.4 1.3 copy-start.9
  454.6 1.5 copy-start.24
  523.4 3.3 copy-start.10
  526.7 26.5 %copy-start.11 = (pred[4,1536]{1,0:T(4,128)(4,1)S(1)}, pred[4,1536]{1,0:T(4,128)(4,1)}, u32[]{:S(2)}) copy-start(pred[4,1536]{1,0:T(4,128)(4,1)} %compare_and_fusion.3) | copy-start | bytes 18436
  563.2 6.4 copy-start.3
  563.2 12.1 %copy-start.13 = (s32[4]{0:T(128)S(1)}, s32[4]{0:T(128)}, u32[]{:S(2)}) copy-start(s32[4]{0:T(128)} %param.21) | copy-start | bytes 52
  563.2 12.1 %copy-start.23 = (s32[4]{0:T(128)S(1)}, s32[4]{0:T(128)}, u32[]{:S(2)}) copy-start(s32[4]{0:T(128)} %param.22) | copy-start | bytes 52
  563.2 12.3 %copy-start.18 = (s32[4]{0:T(128)S(1)}, s32[4]{0:T(128)}, u32[]{:S(2)}) copy-start(s32[4]{0:T(128)} %copy-done.17) | copy-start | bytes 52
  563.2 127.2 %all-to-all-start.1 = ((bf16[4,1536,896]{2,1,0:T(8,128)(2,1)}), bf16[4,1536,896]{2,1,0:T(8,128)(2,1)}, u32[]{:S(2)}, u32[]{:S(2)}) async-start(bf16[4,1536,896]{2,1,0:T(8,128)(2,1)} %broadcast_select_fusion.1), calls=%async_computation.1 | async-start | bytes 22020096 | tf_op jit(solution)/shard_map/all_to_all | solution.py:89
  690.5 27.2 %copy-start.1 = (bf16[14,64,896]{2,1,0:T(8,128)(2,1)S(1)}, bf16[14,64,896]{2,1,0:T(8,128)(2,1)}, u32[]{:S(2)}) copy-start(bf16[14,64,896]{2,1,0:T(8,128)(2,1)} %param.31) | copy-start | bytes 4816900
where the time goes:
time: 722 us; the launch traced here: 718 us
  matrix products  265 us (37%)
  waiting for transfers between devices  234 us (32%)
  local copies, waits for them, and re-layouts  158 us (22%)
  other arithmetic  47 us (7%)
  starting transfers between devices  13.2 us (2%)
    all_to_all x1, waiting for transfers between devices, per_device(): lax.all_to_all(send_buf, 'sp', 0, 0, tiled=True)  119 us
    all_to_all x1, waiting for transfers between devices, per_device(): lax.all_to_all(back_buf, 'sp', 0, 0, tiled=True)  115 us
    sub x12, matrix products, one_block(): jax.nn.softmax(jnp.where(allowed, scores, -1e+30), axis=-1)  104 us
    dot_general x12, matrix products, one_block(): jnp.einsum('kgqs,skd->qkgd', probs_bf, v_proj, preferred_element_type=jnp...  80.4 us
    dot_general x1, matrix products, layer(): jnp.dot(hidden_act, w_down, preferred_element_type=jnp.float32)  44 us
    gather x2, local copies, waits for them, and re-layouts, per_device(): jnp.take(tok_perm, send_idx)  34.3 us
    gather x1, local copies, waits for them, and re-layouts, per_device(): jnp.take(hidden, jnp.take(tok_perm, send_idx), axis=0)  32.5 us
    gather x1, local copies, waits for them, and re-layouts, per_device(): jnp.take(layer_rows, back_idx, axis=0).reshape(group_devs, n_cap, model_dim)  26.5 us
  transfers between devices with their start and end apart: 2, of which 2 were waited for; matrix products, arithmetic and copies ran while one was open for 1% of the time, Pallas kernels for 0%

commit v1 on v0

v1 whole, which is shorter than its diff:
```python
import functools

import jax
import jax.numpy as jnp
from jax import lax
from jax.experimental import pallas as pl
from jax.experimental.pallas import tpu as pltpu
from jax.sharding import PartitionSpec as P

ROPE_BASE = 500000.0
NORM_EPS = 1e-5
ROWS = 512
QB = 256
FT = 256


def norm_rows(rows_f, gain):
    inv = lax.rsqrt(jnp.mean(rows_f * rows_f, axis=-1, keepdims=True) + NORM_EPS)
    return (rows_f * inv * gain).astype(jnp.bfloat16)


def rope_pair(x, cos_t, sin_t, first_half):
    swapped = jnp.where(first_half, pltpu.roll(x, 96, 1), pltpu.roll(x, 32, 1))
    return x * cos_t + swapped * sin_t


def dot_t(a, b):
    return lax.dot_general(a, b, (((1,), (1,)), ((), ())), preferred_element_type=jnp.float32)


def dot_n(a, b):
    return jnp.dot(a, b, preferred_element_type=jnp.float32)


def layer_kernel(maxs_ref, r_ref, start_ref, cos_ref, sin_ref, ga_ref, gm_ref, wq_h, wk_h, wv_h, wo_h, wg_h, wu_h, wd_h, out_ref,
                 q_s, k_s, v_s, o_s, h_s, m_s, wq_s, wk_s, wv_s, wo_s, wg_s, wu_s, wd_s, sems):
    n_rows, dim = r_ref.shape
    n_pairs = dim // 128
    ff = wg_s.shape[1]
    loads = [pltpu.make_async_copy(a, b, sems.at[i]) for i, (a, b) in enumerate(
        [(wq_h, wq_s), (wk_h, wk_s), (wv_h, wv_s), (wo_h, wo_s), (wg_h, wg_s), (wu_h, wu_s), (wd_h, wd_s)])]
    for c in loads:
        c.start()
    for c in loads[:3]:
        c.wait()
    gain_a = ga_ref[...].astype(jnp.float32)
    gain_m = gm_ref[...].astype(jnp.float32)

    @pl.loop(0, n_rows // QB)
    def _qkv(b):
        rows = pl.ds(pl.multiple_of(b * QB, QB), QB)
        lane = lax.broadcasted_iota(jnp.int32, (QB, 128), 1)
        first_half = lane % 64 < 32
        low = lane < 64
        h = norm_rows(r_ref[rows, :].astype(jnp.float32), gain_a)
        cos_t = cos_ref[rows, :]
        sin_t = sin_ref[rows, :]
        q = dot_t(h, wq_s[...])
        for p in range(n_pairs):
            qp = rope_pair(q[:, 128 * p:128 * (p + 1)], cos_t, sin_t, first_half)
            q_s[p, rows, :] = (qp.astype(jnp.bfloat16) * 0.125).astype(jnp.bfloat16)
        k = rope_pair(dot_t(h, wk_s[...]), cos_t, sin_t, first_half)
        v = dot_t(h, wv_s[...])
        for s, x in ((k_s, k), (v_s, v)):
            other = pltpu.roll(x, 64, 1)
            s[0, rows, :] = jnp.where(low, x, other).astype(jnp.bfloat16)
            s[1, rows, :] = jnp.where(low, other, x).astype(jnp.bfloat16)

    for c in range(n_rows // QB):
        length = (c + 1) * QB
        row = c * QB + lax.broadcasted_iota(jnp.int32, (QB, QB), 0)
        col = c * QB + lax.broadcasted_iota(jnp.int32, (QB, QB), 1)
        start = start_ref[c * QB:(c + 1) * QB, :]
        low_q = lax.broadcasted_iota(jnp.int32, (QB, 128), 1) < 64

        def heads(p, masked):
            outs = []
            qp = q_s[p, c * QB:(c + 1) * QB, :]
            for half in range(2):
                g = (2 * p + half) // 7
                qh = jnp.where(low_q if half == 0 else ~low_q, qp, jnp.zeros_like(qp))
                s = dot_t(qh, k_s[g, :length, :])
                diag = jnp.where((col >= start) & (col <= row), s[:, c * QB:], -1e30)
                if c == 0:
                    s = diag
                else:
                    body = s[:, :c * QB]
                    if masked:
                        body_col = lax.broadcasted_iota(jnp.int32, (QB, c * QB), 1)
                        body = jnp.where(body_col >= start, body, -1e30)
                    s = jnp.concatenate([body, diag], axis=1)
                top = jnp.max(s, axis=1, keepdims=True)
                e = jnp.exp(s - top)
                total = jnp.sum(e, axis=1, keepdims=True)
                outs.append(dot_n(e.astype(jnp.bfloat16), v_s[g, :length, :]) / total)
            o_s[c * QB:(c + 1) * QB, pl.ds(pl.multiple_of(p * 128, 128), 128)] = jnp.where(low_q, outs[0], outs[1]).astype(jnp.bfloat16)

        if c == 0:
            @pl.loop(0, n_pairs)
            def _pair(p):
                heads(p, False)
        else:
            has_start = maxs_ref[c] > 0

            @pl.when(has_start)
            def _masked():
                @pl.loop(0, n_pairs)
                def _pair(p):
                    heads(p, True)

            @pl.when(jnp.logical_not(has_start))
            def _plain():
                @pl.loop(0, n_pairs)
                def _pair(p):
                    heads(p, False)

    for c in loads[3:]:
        c.wait()

    @pl.loop(0, n_rows // ROWS)
    def _mlp(b):
        rows = pl.ds(pl.multiple_of(b * ROWS, ROWS), ROWS)
        attn = dot_n(o_s[rows, :], wo_s[...]).astype(jnp.bfloat16)
        z = (r_ref[rows, :].astype(jnp.float32) + attn.astype(jnp.float32)).astype(jnp.bfloat16)
        out_ref[rows, :] = z
        h_s[...] = norm_rows(z.astype(jnp.float32), gain_m)
        for t in range(ff // FT):
            cols = slice(t * FT, (t + 1) * FT)
            gate = dot_n(h_s[...], wg_s[:, cols])
            up = dot_n(h_s[...], wu_s[:, cols])
            m_s[:, cols] = (gate / (1.0 + jnp.exp(-gate)) * up).astype(jnp.bfloat16)
        down = dot_n(m_s[...], wd_s[...]).astype(jnp.bfloat16)
        out_ref[rows, :] = (out_ref[rows, :].astype(jnp.float32) + down.astype(jnp.float32)).astype(jnp.bfloat16)


def layer(dest_rows, positions, g_attn, w_q, w_k, w_v, w_o, g_mlp, w_gate, w_up, w_down):
    n_rows, dim = dest_rows.shape
    head_dim = w_q.shape[2]
    half_dim = head_dim // 2
    ff = w_gate.shape[1]
    inv_freq = jnp.power(jnp.float32(ROPE_BASE), -2.0 * jnp.arange(half_dim, dtype=jnp.float32) / head_dim)
    angles = positions.astype(jnp.float32)[:, None] * inv_freq[None, :]
    cos_t = jnp.cos(angles)
    sin_t = jnp.sin(angles)
    cos_t = jnp.concatenate([cos_t, cos_t, cos_t, cos_t], axis=1)
    sin_t = jnp.concatenate([-sin_t, sin_t, -sin_t, sin_t], axis=1)
    start = jnp.arange(n_rows, dtype=jnp.int32) - positions
    max_start = jnp.max(start.reshape(n_rows // QB, QB), axis=1)
    wq_t = jnp.transpose(w_q, (1, 2, 0)).reshape(dim, dim)
    wk_t = jnp.transpose(w_k, (1, 2, 0)).reshape(128, dim)
    wv_t = jnp.transpose(w_v, (1, 2, 0)).reshape(128, dim)
    wo_t = w_o.reshape(dim, dim)
    vm = pl.BlockSpec(memory_space=pltpu.VMEM)
    hb = pl.BlockSpec(memory_space=pl.ANY)
    bf = jnp.bfloat16
    return pl.pallas_call(
        layer_kernel,
        out_shape=jax.ShapeDtypeStruct((n_rows, dim), bf),
        in_specs=[pl.BlockSpec(memory_space=pltpu.SMEM)] + [vm] * 6 + [hb] * 7,
        out_specs=vm,
        scratch_shapes=[
            pltpu.VMEM((dim // 128, n_rows, 128), bf), pltpu.VMEM((2, n_rows, 128), bf), pltpu.VMEM((2, n_rows, 128), bf),
            pltpu.VMEM((n_rows, dim), bf), pltpu.VMEM((ROWS, dim), bf), pltpu.VMEM((ROWS, ff), bf),
            pltpu.VMEM((dim, dim), bf), pltpu.VMEM((128, dim), bf), pltpu.VMEM((128, dim), bf), pltpu.VMEM((dim, dim), bf),
            pltpu.VMEM((dim, ff), bf), pltpu.VMEM((dim, ff), bf), pltpu.VMEM((ff, dim), bf),
            pltpu.SemaphoreType.DMA((7,))],
        compiler_params=pltpu.CompilerParams(vmem_limit_bytes=66000000),
        cost_estimate=pl.CostEstimate(flops=60_000_000_000, bytes_accessed=40_000_000, transcendentals=0),
        name="layer",
    )(max_start, dest_rows, start[:, None], cos_t, sin_t, g_attn[None, :], g_mlp[None, :], wq_t, wk_t, wv_t, wo_t, w_gate, w_up, w_down)


def solution(mesh):
    row_spec = P(('dp', 'sp'), None)
    vec_spec = P(('dp', 'sp'))
    rep_spec = P()

    def per_device(hidden, tok_perm, send_off, send_len, recv_off, recv_len, recv_doc, recv_pos, g_attn, w_q, w_k, w_v, w_o, g_mlp, w_gate, w_up, w_down):
        n_tok, model_dim = hidden.shape
        n_cap = recv_doc.shape[0]
        group_devs = send_off.shape[0]
        zero_val = jnp.zeros((), hidden.dtype)
        pair_row = jnp.arange(n_cap)[None, :]
        dev_base = jnp.arange(group_devs)[None, :] * n_cap
        send_idx = jnp.minimum(send_off[:, None] + pair_row, n_tok - 1).reshape(-1)
        send_buf = jnp.take(hidden, jnp.take(tok_perm, send_idx), axis=0).reshape(group_devs, n_cap, model_dim)
        recv_buf = lax.all_to_all(send_buf, 'sp', 0, 0, tiled=True).reshape(group_devs * n_cap, model_dim)
        slot_idx = jnp.arange(n_cap)[:, None]
        in_run = (slot_idx >= recv_off[None, :]) & (slot_idx < (recv_off + recv_len)[None, :])
        flat_pos = jnp.sum(jnp.where(in_run, dev_base + slot_idx - recv_off[None, :], 0), axis=1)
        dest_rows = jnp.take(recv_buf, flat_pos, axis=0)
        layer_rows = layer(dest_rows, recv_pos, g_attn, w_q, w_k, w_v, w_o, g_mlp, w_gate, w_up, w_down)
        back_idx = jnp.minimum(recv_off[:, None] + pair_row, n_cap - 1).reshape(-1)
        back_buf = jnp.take(layer_rows, back_idx, axis=0).reshape(group_devs, n_cap, model_dim)
        back_recv = lax.all_to_all(back_buf, 'sp', 0, 0, tiled=True).reshape(group_devs * n_cap, model_dim)
        inv_perm = jnp.argsort(tok_perm)[:, None]
        in_back = (inv_perm >= send_off[None, :]) & (inv_perm < (send_off + send_len)[None, :])
        back_pos = jnp.sum(jnp.where(in_back, dev_base + inv_perm - send_off[None, :], 0), axis=1)
        was_sent = jnp.any(in_back, axis=1)
        return jnp.where(was_sent[:, None], jnp.take(back_recv, back_pos, axis=0), zero_val)

    return jax.shard_map(per_device, mesh=mesh, in_specs=(row_spec,) + (vec_spec,) * 7 + (rep_spec,) * 9, out_specs=row_spec, check_vma=False)
```

time: 722 us -> 541 us (0.75)
  the two profiles are of different devices: /device:TPU:0 before, /device:TPU:4 now
where the time goes in v1:
time: 541 us; the launch traced here: 532 us
  waiting for transfers between devices  227 us (42%)
  local copies, waits for them, and re-layouts  133 us (25%)
  Pallas kernels  117 us (22%)
  other arithmetic  41.9 us (8%)
  starting transfers between devices  12.5 us (2%)
    pallas_call x1, Pallas kernels, layer(): pl.pallas_call(layer_kernel, out_shape=jax.ShapeDtypeStruct((n_rows, dim)...  117 us
    all_to_all x1, waiting for transfers between devices, per_device(): lax.all_to_all(back_buf, 'sp', 0, 0, tiled=True)  115 us
    all_to_all x1, waiting for transfers between devices, per_device(): lax.all_to_all(send_buf, 'sp', 0, 0, tiled=True)  112 us
    gather x2, local copies, waits for them, and re-layouts, per_device(): jnp.take(tok_perm, send_idx)  34.3 us
    gather x1, local copies, waits for them, and re-layouts, per_device(): jnp.take(hidden, jnp.take(tok_perm, send_idx), axis=0)  32.5 us
    gather x1, local copies, waits for them, and re-layouts, per_device(): jnp.take(layer_rows, back_idx, axis=0).reshape(group_devs, n_cap, model_dim)  31.4 us
    gather x1, local copies, waits for them, and re-layouts, per_device(): jnp.take(back_recv, back_pos, axis=0)  20.6 us
    gather x1, local copies, waits for them, and re-layouts, per_device(): dest_rows = jnp.take(recv_buf, flat_pos, axis=0)  12 us
  transfers between devices with their start and end apart: 2, of which 2 were waited for; matrix products, arithmetic and copies ran while one was open for 3% of the time, Pallas kernels for 0%

profile of v1, /device:TPU:4, one launch (start us, length us, event | category | flops | bytes accessed | tf_op | source)
XLA Modules:
  0.0 532.0 jit_solution(5693900193378540008)
XLA Ops:
  0.0 0.7 fusion.1
  0.8 0.0 copy-done
  0.8 0.0 copy-start.2
  0.8 34.3 %gather_fusion = s32[6144]{0:T(1024)S(1)} fusion(s32[3072]{0:T(1024)S(1)} %copy-done, s32[6144]{0:T(1024)S(1)} %broadcast_clamp_fusion.2), kind=kCustom, calls=%fused_computation | custom fusion | bytes 73728 | tf_op jit(solution)/shard_map/jit(_take)/gather | solution.py:186
  35.2 0.1 compare_select_fusion.1
  35.3 0.1 compare_and_fusion.1
  35.4 32.5 %gather_fusion.1 = bf16[6144,896]{1,0:T(8,128)(2,1)} fusion(bf16[3072,896]{1,0:T(8,128)(2,1)} %param.17, s32[6144]{0:T(1024)S(1)} %broadcast_clamp_fusion.1), kind=kCustom, calls=%fused_computation.1 | custom fusion | bytes 22044672 | tf_op jit(solution)/shard_map/jit(_take)/gather | solution.py:186
  67.8 10.0 %broadcast_select_fusion = bf16[4,1536,896]{2,1,0:T(8,128)(2,1)} fusion(bf16[4,1536,896]{2,1,0:T(8,128)(2,1)} %bitcast.31, pred[4,1536]{1,0:T(4,128)(4,1)S(1)} %compare_and_fusion.1), kind=kLoop, calls=%fused_computation.5 | loop fusion | flops 5505024 | bytes 22026240 | tf_op jit(solution)/shard_map/jit(_take)/select_n | solution.py:186
  77.8 0.0 copy-start.8
  77.8 6.3 %all-to-all-start = ((bf16[4,1536,896]{2,1,0:T(8,128)(2,1)}), bf16[4,1536,896]{2,1,0:T(8,128)(2,1)}, u32[]{:S(2)}, u32[]{:S(2)}) async-start(bf16[4,1536,896]{2,1,0:T(8,128)(2,1)} %broadcast_select_fusion), calls=%async_computation | async-start | bytes 22020096 | tf_op jit(solution)/shard_map/all_to_all | solution.py:187
  84.2 1.2 broadcast_in_dim.106.start_ref
  85.3 0.6 broadcast_in_dim.102.ga_ref
  85.9 0.6 broadcast_in_dim.103.gm_ref
  86.5 0.1 fusion.2
  86.6 0.6 reduce_max.9.maxs_ref
  87.3 0.1 select_reduce_fusion.1
  87.5 2.8 fusion
  90.3 2.5 pad_maximum_fusion
  92.8 0.1 compare_and_fusion.2
  92.9 112.2 %all-to-all-done = bf16[4,1536,896]{2,1,0:T(8,128)(2,1)} async-done(((bf16[4,1536,896]{2,1,0:T(8,128)(2,1)}), bf16[4,1536,896]{2,1,0:T(8,128)(2,1)}, u32[]{:S(2)}, u32[]{:S(2)}) %all-to-all-start) | async-done | bytes 11010080 | tf_op jit(solution)/shard_map/all_to_all | solution.py:187
  205.0 12.0 %gather_fusion.2 = bf16[1536,896]{1,0:T(8,128)(2,1)S(1)} fusion(bf16[6144,896]{1,0:T(8,128)(2,1)} %bitcast.4, s32[2048]{0:T(1024)S(1)} %pad_clamp_fusion), kind=kCustom, calls=%fused_computation.2 | custom fusion | bytes 5511168 | tf_op jit(solution)/shard_map/jit(_take)/gather | solution.py:191
  217.1 2.0 broadcast_select_fusion.2.r_ref
  219.0 116.7 %layer.1 = bf16[1536,896]{1,0:T(8,128)(2,1)} custom-call(s32[6]{0:T(128)} %reduce_max.9.maxs_ref, bf16[1536,896]{1,0:T(8,128)(2,1)} %broadcast_select_fusion.2.r_ref, s32[1536,1]{1,0:T(8,128)} %broadcast_in_dim.106.start_ref, f32[1536,128]{1,0:T(8,128)} %get-tuple-element.12.cos_ref, f32[1536,128]{1,0:T(8,128)} %get-tuple-element.13.sin_ref, ...), custom_call_target="tpu_custom_call" | custom-call | flops 60000002048 | bytes 40000000 | tf_op jit(solution)/shard_map/layer/pallas_call | solution.py:156
  335.8 31.4 %gather_fusion.3 = bf16[6144,896]{1,0:T(8,128)(2,1)} fusion(bf16[1536,896]{1,0:T(8,128)(2,1)} %layer.1, s32[6144]{0:T(1024)S(1)} %broadcast_clamp_fusion), kind=kCustom, calls=%fused_computation.3 | custom fusion | bytes 22044672 | tf_op jit(solution)/shard_map/jit(_take)/gather | solution.py:194
  367.1 10.3 %broadcast_select_fusion.1 = bf16[4,1536,896]{2,1,0:T(8,128)(2,1)} fusion(bf16[4,1536,896]{2,1,0:T(8,128)(2,1)} %bitcast.30, pred[4,1536]{1,0:T(4,128)(4,1)S(1)} %compare_and_fusion.2), kind=kLoop, calls=%fused_computation.6 | loop fusion | flops 5505024 | bytes 22026240 | tf_op jit(solution)/shard_map/jit(_take)/select_n | solution.py:194
  377.4 6.2 %all-to-all-start.1 = ((bf16[4,1536,896]{2,1,0:T(8,128)(2,1)}), bf16[4,1536,896]{2,1,0:T(8,128)(2,1)}, u32[]{:S(2)}, u32[]{:S(2)}) async-start(bf16[4,1536,896]{2,1,0:T(8,128)(2,1)} %broadcast_select_fusion.1), calls=%async_computation.1 | async-start | bytes 22020096 | tf_op jit(solution)/shard_map/all_to_all | solution.py:195
  383.7 5.8 %sort.17 = (s32[3072]{0:T(1024)}, s32[3072]{0:T(1024)S(1)}) sort(s32[3072]{0:T(1024)S(1)} %copy-done.1, s32[3072]{0:T(1024)S(1)} %iota.28), dimensions={0}, to_apply=%region_0.1 | sort | flops 36864 | bytes 49152 | tf_op jit(solution)/shard_map/jit(argsort)/sort | solution.py:196
  389.4 0.1 fusion.5
  389.5 0.1 select_reduce_fusion
  389.7 114.8 %all-to-all-done.1 = bf16[4,1536,896]{2,1,0:T(8,128)(2,1)} async-done(((bf16[4,1536,896]{2,1,0:T(8,128)(2,1)}), bf16[4,1536,896]{2,1,0:T(8,128)(2,1)}, u32[]{:S(2)}, u32[]{:S(2)}) %all-to-all-start.1) | async-done | bytes 11010080 | tf_op jit(solution)/shard_map/all_to_all | solution.py:195
  504.5 20.6 %gather_fusion.4 = bf16[3072,896]{1,0:T(8,128)(2,1)} fusion(bf16[6144,896]{1,0:T(8,128)(2,1)} %bitcast.14, s32[3072]{0:T(1024)S(1)} %broadcast_clamp_fusion.3), kind=kCustom, calls=%fused_computation.4 | custom fusion | bytes 11022336 | tf_op jit(solution)/shard_map/jit(_take)/gather | solution.py:200
  525.2 6.4 %select_select_fusion = bf16[3072,896]{1,0:T(8,128)(2,1)} fusion(bf16[3072,896]{1,0:T(8,128)(2,1)} %gather_fusion.4, pred[3072]{0:T(1024)(128)(4,1)S(1)} %compare_and_fusion.3, pred[3072]{0:T(1024)(128)(4,1)S(1)} %fusion.5), kind=kLoop, calls=%fused_computation.7 | loop fusion | flops 5505024 | bytes 11016192 | tf_op jit(solution)/shard_map/jit(_where)/select_n | solution.py:200
  (38 shorter events, 0.3 us)
Async XLA Ops:
  0.0 0.8 copy-start
  0.8 34.4 %copy-start.2 = (s32[4]{0:T(128)S(1)}, s32[4]{0:T(128)}, u32[]{:S(2)}) copy-start(s32[4]{0:T(128)} %param.19) | copy-start | bytes 52
  77.8 6.3 %copy-start.4 = (s32[1536]{0:T(1024)S(1)}, s32[1536]{0:T(1024)}, u32[]{:S(2)}) copy-start(s32[1536]{0:T(1024)} %param.23) | copy-start | bytes 18436
  77.8 7.5 %copy-start.6 = (bf16[896]{0:T(1024)(128)(2,1)S(1)}, bf16[896]{0:T(1024)(128)(2,1)}, u32[]{:S(2)}) copy-start(bf16[896]{0:T(1024)(128)(2,1)} %param.24) | copy-start | bytes 5380
  77.8 8.1 %copy-start.7 = (bf16[896]{0:T(1024)(128)(2,1)S(1)}, bf16[896]{0:T(1024)(128)(2,1)}, u32[]{:S(2)}) copy-start(bf16[896]{0:T(1024)(128)(2,1)} %param.29) | copy-start | bytes 5380
  77.8 8.7 %copy-start.5 = (s32[4]{0:T(128)S(1)}, s32[4]{0:T(128)}, u32[]{:S(2)}) copy-start(s32[4]{0:T(128)} %param.21) | copy-start | bytes 52
  77.8 8.7 %copy-start.8 = (s32[4]{0:T(128)S(1)}, s32[4]{0:T(128)}, u32[]{:S(2)}) copy-start(s32[4]{0:T(128)} %param.22) | copy-start | bytes 52
  77.8 127.2 %all-to-all-start = ((bf16[4,1536,896]{2,1,0:T(8,128)(2,1)}), bf16[4,1536,896]{2,1,0:T(8,128)(2,1)}, u32[]{:S(2)}, u32[]{:S(2)}) async-start(bf16[4,1536,896]{2,1,0:T(8,128)(2,1)} %broadcast_select_fusion), calls=%async_computation | async-start | bytes 22020096 | tf_op jit(solution)/shard_map/all_to_all | solution.py:187
  377.4 6.3 %copy-start.1 = (s32[3072]{0:T(1024)S(1)}, s32[3072]{0:T(1024)}, u32[]{:S(2)}) copy-start(s32[3072]{0:T(1024)} %param.18) | copy-start | bytes 36868
  377.4 12.0 %copy-start.3 = (s32[4]{0:T(128)S(1)}, s32[4]{0:T(128)}, u32[]{:S(2)}) copy-start(s32[4]{0:T(128)} %param.19) | copy-start | bytes 52
  377.4 12.0 %copy-start.9 = (s32[4]{0:T(128)S(1)}, s32[4]{0:T(128)}, u32[]{:S(2)}) copy-start(s32[4]{0:T(128)} %param.20) | copy-start | bytes 52
  377.4 127.1 %all-to-all-start.1 = ((bf16[4,1536,896]{2,1,0:T(8,128)(2,1)}), bf16[4,1536,896]{2,1,0:T(8,128)(2,1)}, u32[]{:S(2)}, u32[]{:S(2)}) async-start(bf16[4,1536,896]{2,1,0:T(8,128)(2,1)} %broadcast_select_fusion.1), calls=%async_computation.1 | async-start | bytes 22020096 | tf_op jit(solution)/shard_map/all_to_all | solution.py:195
